TPU v7x, 32 devices: a whole 2x2x4 slice. The times are simulated.
32 devices in a mesh: dp: 8 (over z, x), tp: 4 (over y, core).
Axes of the slice: x: 2, y: 2, z: 4, core: 2. Of those that a mesh axis runs over, the one named last changes fastest.
Arguments:
- main: bfloat16 [16512, 1152], P('dp', 'tp'), may hold values from -6 to 6
- long_skip: bfloat16 [16512, 1152], P('dp', 'tp'), may hold values from -6 to 6
- cotangent: bfloat16 [16512, 1152], P('dp', 'tp'), may hold values from -6 to 6
- timesteps: int32 [64], P('dp'), may hold values from 0 to 999
- loss_codes: int32 [64], P('dp'), may hold values from 0 to 7
- code_weights: float32 [8], replicated, may hold values from 0.25 to 4
- item_counts: int32 [8], P('dp'), may hold values from 4 to 8, as said below
- w_skip_main: bfloat16 [1152, 1152], P('tp'), may hold values from -0.125 to 0.125
- w_skip_long: bfloat16 [1152, 1152], P('tp'), may hold values from -0.125 to 0.125
- b_skip: float32 [1152], P('tp'), may hold values from -3 to 3
- ln1_gain: float32 [1152], P('tp'), may hold values from 0.25 to 1.75
- ln1_bias: float32 [1152], P('tp'), may hold values from -2.4 to 2.4
- w_qkv: bfloat16 [3, 1152, 1152], P(None, None, 'tp'), may hold values from -0.1875 to 0.1875
- w_proj: bfloat16 [1152, 1152], P('tp'), may hold values from -1.5 to 1.5
- b_proj: float32 [1152], P('tp'), may hold values from -3 to 3
- ln2_gain: float32 [1152], P('tp'), may hold values from 0.25 to 1.75
- ln2_bias: float32 [1152], P('tp'), may hold values from -2.4 to 2.4
- w_up: bfloat16 [1152, 4608], P(None, 'tp'), may hold values from -0.1875 to 0.1875
- b_up: float32 [4608], P('tp'), may hold values from -3 to 3
- w_down: bfloat16 [4608, 1152], P('tp'), may hold values from -0.09375 to 0.09375
- b_down: float32 [1152], P('tp'), may hold values from -3 to 3
Outputs:
- out: bfloat16 [16512, 1152], P('dp', 'tp')
- d_main: bfloat16 [16512, 1152], P('dp', 'tp')
- d_long: bfloat16 [16512, 1152], P('dp', 'tp')
- g_w_skip_main: float32 [1152, 1152], P('tp')
- g_w_skip_long: float32 [1152, 1152], P('tp')
- g_b_skip: float32 [1152], P('tp')
- g_ln1_gain: float32 [1152], P('tp')
- g_ln1_bias: float32 [1152], P('tp')
- g_w_qkv: float32 [3, 1152, 1152], P(None, None, 'tp')
- g_w_proj: float32 [1152, 1152], P('tp')
- g_b_proj: float32 [1152], P('tp')
- g_ln2_gain: float32 [1152], P('tp')
- g_ln2_bias: float32 [1152], P('tp')
- g_w_up: float32 [1152, 4608], P(None, 'tp')
- g_b_up: float32 [4608], P('tp')
- g_w_down: float32 [4608, 1152], P('tp')
- g_b_down: float32 [1152], P('tp')
Inputs may be any that keep to these rules, and one draw needn't show every extreme that they name: `item_counts`: each batch group holds 4 to 8 items; some group is full and some holds exactly 4.
All inputs are finite; a program needn't handle non-finite values.
Results may differ from a plain program's by a relative error of at most 0.02.
Values may be sent and summed in bfloat16 or wider, within the bound.
A program may use at most 192 MiB of HBM per device.

v0:
```python
import math
import jax
import jax.numpy as jnp
from jax import lax
from jax.sharding import PartitionSpec as P

HEAD = 72
SEQ = 258
TSTEPS = 1000
EPSILON = 1e-06
ROOT_HALF = 0.7071067811865476
DENSITY_SCALE = 0.3989422804014327


def item_factors(timesteps, loss_codes, code_weights, group_items):
    steps_float = timesteps.astype(jnp.float32)
    phase = (steps_float / TSTEPS + 0.008) / 1.008 * (math.pi / 2.0)
    cosine = jnp.cos(phase)
    signal = cosine * cosine
    weight = jnp.minimum(1.0, 5.0 * (1.0 - signal) / signal)
    picks = (
        loss_codes[:, None] == jnp.arange(code_weights.shape[0], dtype=jnp.int32)[None, :]
    ).astype(jnp.float32)
    coded = jnp.sum(picks * code_weights[None, :], axis=1)
    valid = (jnp.arange(timesteps.shape[0], dtype=jnp.int32) < group_items).astype(jnp.float32)
    return (weight * coded * valid, valid)


def layer_norm(stream, gain, bias, width):
    totals, squares = lax.psum((jnp.sum(stream, 0), jnp.sum(stream * stream, 0)), "tp")
    mean = totals / width
    rstd = lax.rsqrt(squares / width - mean * mean + EPSILON)
    normed = (stream - mean[None, :]) * rstd[None, :]
    rounded = (normed * gain[:, None] + bias[:, None]).astype(jnp.bfloat16)
    return (normed, rstd, lax.all_gather(rounded, "tp", axis=0, tiled=True))


def norm_back(d_normed, normed, rstd, gain, width):
    g_gain = jnp.sum(d_normed * normed, 1)
    g_bias = jnp.sum(d_normed, 1)
    scaled = d_normed * gain[:, None]
    first, second = lax.psum((jnp.sum(scaled, 0), jnp.sum(scaled * normed, 0)), "tp")
    back = rstd[None, :] * (scaled - first[None, :] / width - normed * second[None, :] / width)
    return (back, g_gain, g_bias)


def reduce_back(term, local_width):
    return lax.psum_scatter(
        term(jnp.int32(0), lax.axis_size("tp") * local_width).astype(jnp.bfloat16),
        "tp",
        scatter_dimension=0,
        tiled=True,
    ).astype(jnp.float32)


def fold_back(shard, pairs):
    piece = lax.all_gather(shard, "tp", axis=0, tiled=True)
    new_acts = tuple(
        (
            jnp.einsum("fc,ct->ft", weight, piece, preferred_element_type=jnp.float32)
            for weight, acts in pairs
        )
    )
    new_weights = tuple(
        (
            jnp.einsum("ft,ct->fc", acts, piece, preferred_element_type=jnp.float32)
            for weight, acts in pairs
        )
    )
    return (new_acts, new_weights)


def split_heads(flat, heads_here):
    pair_count = flat.shape[1] // (2 * SEQ)
    shaped = flat.reshape(heads_here, HEAD, pair_count, 2, SEQ)
    return jnp.moveaxis(shaped, 2, 0)


def join_heads(blocks):
    moved = jnp.moveaxis(blocks, 0, 2)
    return moved.reshape(moved.shape[0] * moved.shape[1], -1)


def attend(block):
    query_rows, key_rows, value_rows = block
    scale = 1.0 / math.sqrt(HEAD)
    scores = (
        jnp.einsum("hdbi,hdbj->hbij", query_rows, key_rows, preferred_element_type=jnp.float32)
        * scale
    )
    peak = jnp.max(scores, axis=-1, keepdims=True)
    logsum = peak + jnp.log(jnp.sum(jnp.exp(scores - peak), axis=-1, keepdims=True))
    probs = jnp.exp(scores - logsum).astype(jnp.bfloat16)
    attended = jnp.einsum("hbij,hdbj->hdbi", probs, value_rows, preferred_element_type=jnp.float32)
    return (attended.astype(jnp.bfloat16), logsum[..., 0])


def attend_back(block):
    query_rows, key_rows, value_rows, logsum, d_attended = block
    scale = 1.0 / math.sqrt(HEAD)
    scores = (
        jnp.einsum("hdbi,hdbj->hbij", query_rows, key_rows, preferred_element_type=jnp.float32)
        * scale
    )
    probs = jnp.exp(scores - logsum[..., None])
    probs_low = probs.astype(jnp.bfloat16)
    d_probs = jnp.einsum(
        "hdbi,hdbj->hbij", d_attended, value_rows, preferred_element_type=jnp.float32
    )
    delta = jnp.sum(probs * d_probs, axis=-1, keepdims=True)
    d_scores = (probs * (d_probs - delta)).astype(jnp.bfloat16)
    d_query = (
        jnp.einsum("hbij,hdbj->hdbi", d_scores, key_rows, preferred_element_type=jnp.float32)
        * scale
    )
    d_key = (
        jnp.einsum("hbij,hdbi->hdbj", d_scores, query_rows, preferred_element_type=jnp.float32)
        * scale
    )
    d_value = jnp.einsum(
        "hbij,hdbi->hdbj", probs_low, d_attended, preferred_element_type=jnp.float32
    )
    return (d_query.astype(jnp.bfloat16), d_key.astype(jnp.bfloat16), d_value.astype(jnp.bfloat16))


def body(
    main,
    long_skip,
    cotangent,
    timesteps,
    loss_codes,
    code_weights,
    item_counts,
    w_skip_main,
    w_skip_long,
    b_skip,
    ln1_gain,
    ln1_bias,
    w_qkv,
    w_proj,
    b_proj,
    ln2_gain,
    ln2_bias,
    w_up,
    b_up,
    w_down,
    b_down,
):
    local_width = main.shape[1]
    width = w_skip_main.shape[1]
    heads_here = local_width // HEAD
    item_scale, valid = item_factors(timesteps, loss_codes, code_weights, item_counts[0])
    row_scale = jnp.repeat(item_scale, SEQ)
    row_valid = jnp.repeat(valid, SEQ)
    main_cols = main.T
    long_cols = long_skip.T
    stream = (
        lax.psum_scatter(
            jnp.einsum("dc,dt->ct", w_skip_main, main_cols, preferred_element_type=jnp.float32)
            + jnp.einsum("dc,dt->ct", w_skip_long, long_cols, preferred_element_type=jnp.float32),
            "tp",
            scatter_dimension=0,
            tiled=True,
        )
        + b_skip[:, None]
    )
    normed_one, rstd_one, full_one = layer_norm(stream, ln1_gain, ln1_bias, width)
    qkv = jnp.einsum("edc,dt->ect", w_qkv, full_one, preferred_element_type=jnp.float32).astype(
        jnp.bfloat16
    )
    query_blocks = split_heads(qkv[0], heads_here)
    key_blocks = split_heads(qkv[1], heads_here)
    value_blocks = split_heads(qkv[2], heads_here)
    attended_blocks, logsums = lax.map(attend, (query_blocks, key_blocks, value_blocks))
    attended = join_heads(attended_blocks)
    cols_here = w_proj
    projected = lax.psum_scatter(
        jnp.einsum("rc,rt->ct", cols_here, attended, preferred_element_type=jnp.float32).astype(
            jnp.bfloat16
        ),
        "tp",
        scatter_dimension=0,
        tiled=True,
    ).astype(jnp.float32)
    stream_two = stream + projected + b_proj[:, None]
    normed_two, rstd_two, full_two = layer_norm(stream_two, ln2_gain, ln2_bias, width)
    upward = (
        jnp.einsum("dc,dt->ct", w_up, full_two, preferred_element_type=jnp.float32) + b_up[:, None]
    )
    activated = jax.nn.gelu(upward, approximate=False).astype(jnp.bfloat16)
    cols_here = w_down
    result = (
        stream_two
        + lax.psum_scatter(
            jnp.einsum(
                "fc,ft->ct", cols_here, activated, preferred_element_type=jnp.float32
            ).astype(jnp.bfloat16),
            "tp",
            scatter_dimension=0,
            tiled=True,
        ).astype(jnp.float32)
        + b_down[:, None]
    )
    out = (result * row_valid[None, :]).T.astype(jnp.bfloat16)
    grad_low = (cotangent.T.astype(jnp.float32) * row_scale[None, :]).astype(jnp.bfloat16)
    grad_wide = grad_low.astype(jnp.float32)
    g_b_down = jnp.sum(grad_wide, 1)
    (d_activated,), (g_w_down,) = fold_back(grad_low, ((w_down, activated),))
    cumulative = 0.5 * (1.0 + lax.erf(upward * ROOT_HALF))
    density = jnp.exp(-0.5 * upward * upward) * DENSITY_SCALE
    d_upward = (d_activated * (cumulative + upward * density)).astype(jnp.bfloat16)
    g_b_up = jnp.sum(d_upward.astype(jnp.float32), 1)
    g_w_up = jnp.einsum("dt,ft->df", full_two, d_upward, preferred_element_type=jnp.float32)

    def up_term(start, count_rows):
        return jnp.einsum("cf,ft->ct", w_up, d_upward, preferred_element_type=jnp.float32)

    d_normed_two = reduce_back(up_term, local_width)
    back_two, g_ln2_gain, g_ln2_bias = norm_back(
        d_normed_two, normed_two, rstd_two, ln2_gain, width
    )
    d_stream_two = (back_two + grad_wide).astype(jnp.bfloat16)
    d_stream_wide = d_stream_two.astype(jnp.float32)
    g_b_proj = jnp.sum(d_stream_wide, 1)
    (d_attended,), (g_w_proj,) = fold_back(d_stream_two, ((w_proj, attended),))
    d_attended_blocks = split_heads(d_attended.astype(jnp.bfloat16), heads_here)
    d_queries, d_keys, d_values = lax.map(
        attend_back, (query_blocks, key_blocks, value_blocks, logsums, d_attended_blocks)
    )
    d_qkv = jnp.stack([join_heads(d_queries), join_heads(d_keys), join_heads(d_values)], axis=0)
    g_w_qkv = jnp.einsum("dt,ect->edc", full_one, d_qkv, preferred_element_type=jnp.float32)

    def qkv_term(start, count_rows):
        return jnp.einsum("ecr,ert->ct", w_qkv, d_qkv, preferred_element_type=jnp.float32)

    d_normed_one = reduce_back(qkv_term, local_width)
    back_one, g_ln1_gain, g_ln1_bias = norm_back(
        d_normed_one, normed_one, rstd_one, ln1_gain, width
    )
    d_stream = (back_one + d_stream_wide).astype(jnp.bfloat16)
    g_b_skip = jnp.sum(d_stream.astype(jnp.float32), 1)
    (d_main_cols, d_long_cols), (g_w_main, g_w_long) = fold_back(
        d_stream, ((w_skip_main, main_cols), (w_skip_long, long_cols))
    )
    (
        g_w_main,
        g_w_long,
        g_b_skip,
        g_ln1_gain,
        g_ln1_bias,
        g_w_qkv,
        g_w_proj,
        g_b_proj,
        g_ln2_gain,
        g_ln2_bias,
        g_w_up,
        g_b_up,
        g_w_down,
        g_b_down,
    ) = (
        lax.psum(g_w_main.astype(jnp.bfloat16), "dp").astype(jnp.float32),
        lax.psum(g_w_long.astype(jnp.bfloat16), "dp").astype(jnp.float32),
        lax.psum(g_b_skip.astype(jnp.bfloat16), "dp").astype(jnp.float32),
        lax.psum(g_ln1_gain.astype(jnp.bfloat16), "dp").astype(jnp.float32),
        lax.psum(g_ln1_bias.astype(jnp.bfloat16), "dp").astype(jnp.float32),
        lax.psum(g_w_qkv.astype(jnp.bfloat16), "dp").astype(jnp.float32),
        lax.psum(g_w_proj.astype(jnp.bfloat16), "dp").astype(jnp.float32),
        lax.psum(g_b_proj.astype(jnp.bfloat16), "dp").astype(jnp.float32),
        lax.psum(g_ln2_gain.astype(jnp.bfloat16), "dp").astype(jnp.float32),
        lax.psum(g_ln2_bias.astype(jnp.bfloat16), "dp").astype(jnp.float32),
        lax.psum(g_w_up.astype(jnp.bfloat16), "dp").astype(jnp.float32),
        lax.psum(g_b_up.astype(jnp.bfloat16), "dp").astype(jnp.float32),
        lax.psum(g_w_down.astype(jnp.bfloat16), "dp").astype(jnp.float32),
        lax.psum(g_b_down.astype(jnp.bfloat16), "dp").astype(jnp.float32),
    )
    d_main = d_main_cols.T.astype(jnp.bfloat16)
    d_long = d_long_cols.T.astype(jnp.bfloat16)
    return (
        out,
        d_main,
        d_long,
        g_w_main,
        g_w_long,
        g_b_skip,
        g_ln1_gain,
        g_ln1_bias,
        g_w_qkv,
        g_w_proj,
        g_b_proj,
        g_ln2_gain,
        g_ln2_bias,
        g_w_up,
        g_b_up,
        g_w_down,
        g_b_down,
    )


def solution(mesh):
    return jax.shard_map(
        body,
        mesh=mesh,
        in_specs=(
            P("dp", "tp"),
            P("dp", "tp"),
            P("dp", "tp"),
            P("dp"),
            P("dp"),
            P(),
            P("dp"),
            P("tp", None),
            P("tp", None),
            P("tp"),
            P("tp"),
            P("tp"),
            P(None, None, "tp"),
            P("tp", None),
            P("tp"),
            P("tp"),
            P("tp"),
            P(None, "tp"),
            P("tp"),
            P("tp", None),
            P("tp"),
        ),
        out_specs=(
            P("dp", "tp"),
            P("dp", "tp"),
            P("dp", "tp"),
            P("tp", None),
            P("tp", None),
            P("tp"),
            P("tp"),
            P("tp"),
            P(None, None, "tp"),
            P("tp", None),
            P("tp"),
            P("tp"),
            P("tp"),
            P(None, "tp"),
            P("tp"),
            P("tp", None),
            P("tp"),
        ),
        check_vma=False,
    )
```

profile of v0, /device:TPU:0, one launch (start us, length us, event | category | flops | bytes accessed | tf_op | source)
XLA Modules:
  0.0 1135.2 jit_solution(10548227006924629064)
XLA Ops:
  11.9 6.9 convolution_add_fusion
  18.9 84.4 %reduce-scatter.16.cloned.1.call-done = f32[288,2064]{1,0:T(8,128)} async-done(((f32[1152,2064]{1,0:T(8,128)}), f32[288,2064]{1,0:T(8,128)}) %reduce-scatter.16.cloned.1.call-update) | async-done | bytes 2377744
  109.4 10.3 all-reduce.3
  126.7 39.5 %all-gather.6.cloned.1.call-done = bf16[1152,2064]{1,0:T(8,128)(2,1)} async-done(((bf16[288,2064]{1,0:T(8,128)(2,1)}), bf16[1152,2064]{1,0:T(8,128)(2,1)}) %all-gather.6.cloned.1.call-update) | async-done | bytes 4755472 | tf_op jit(solution)/shard_map/all_gather | solution.py:35
  166.2 8.2 fusion.83
  176.4 6.6 reshape_squeeze.11
  183.0 6.6 reshape_squeeze.10
  203.0 23.4 %while.26 = (s32[]{:T(128)}, bf16[4,4,72,2,258]{4,2,3,1,0:T(8,128)(2,1)}, f32[4,4,2,258]{3,2,1,0:T(2,128)}, bf16[4,4,72,2,258]{4,2,3,1,0:T(8,128)(2,1)}, bf16[4,...) while((s32[]{:T(128)}, bf16[4,4,72,2,258]{4,2,3,1,0:T(8,128)(2,1)}, ...), condition=%wide.region_8.0_spmd, body=%wide.region_5.8_spmd.sunk | while | flops 157770096 | bytes 8231833 | solution.py:174
  242.0 8.4 copy.129
  250.5 50.0 %reduce-scatter.18.cloned.1.call-done = bf16[288,2064]{1,0:T(8,128)(2,1)} async-done(((bf16[1152,2064]{1,0:T(8,128)(2,1)}), bf16[288,2064]{1,0:T(8,128)(2,1)}) %reduce-scatter.18.cloned.1.call-update) | async-done | bytes 1188880
  307.6 10.3 all-reduce.2
  333.6 30.3 %all-gather.8.cloned.1.call-done = bf16[1152,2064]{1,0:T(8,128)(2,1)} async-done(((bf16[288,2064]{1,0:T(8,128)(2,1)}), bf16[1152,2064]{1,0:T(8,128)(2,1)}) %all-gather.8.cloned.1.call-update) | async-done | bytes 4755472 | tf_op jit(solution)/shard_map/all_gather | solution.py:35
  363.9 32.2 %fusion.68 = (bf16[1152,2064]{0,1:T(8,128)(2,1)S(1)}, f32[1152,2064]{0,1:T(8,128)}) fusion(f32[1152]{0:T(1024)S(1)} %copy-done.46, bf16[1152,2064]{1,0:T(8,128)(2,1)} %all-gather.8.cloned.1.call-done, bf16[1152,1152]{1,0:T(8,128)(2,1)S(1)} %copy-done), kind=kOutput, calls=%fused_computation.81 | convolution fusion | flops 5635215360 | bytes 21680640 | tf_op jit(solution)/shard_map/dc,dt->ct/dot_general | solution.py:188
  398.4 8.5 fusion.63
  406.9 8.4 copy.131
  415.3 16.6 %fusion.122 = (bf16[1152]{0:T(1024)(128)(2,1)}, bf16[1152,2064]{0,1:T(8,128)(2,1)S(1)}) fusion(f32[1152,2064]{0,1:T(8,128)} %get-tuple-element.220, bf16[1152,2064]{1,0:T(8,128)(2,1)} %all-gather.10.cloned.1.call-done, bf16[1152,1152]{1,0:T(8,128)(2,1)} %param.44), kind=kOutput, calls=%fused_computation.176 | convolution fusion | flops 5504439296 | bytes 21678336 | tf_op jit(solution)/shard_map/fc,ct->ft/dot_general | solution.py:60
  434.1 8.7 fusion.64
  442.8 8.4 copy.133
  451.4 13.8 %reduce-scatter.20.cloned.1.call-done = bf16[288,2064]{1,0:T(8,128)(2,1)} async-done(((bf16[1152,2064]{1,0:T(8,128)(2,1)}), bf16[288,2064]{1,0:T(8,128)(2,1)}) %reduce-scatter.20.cloned.1.call-update) | async-done | bytes 1188880
  467.8 50.5 %reduce-scatter.22.cloned.1.call-done = bf16[288,2064]{1,0:T(8,128)(2,1)} async-done(((bf16[1152,2064]{1,0:T(8,128)(2,1)}), bf16[288,2064]{1,0:T(8,128)(2,1)}) %reduce-scatter.22.cloned.1.call-update) | async-done | bytes 1188880
  526.9 10.3 all-reduce.1
  544.9 39.8 %all-gather.12.cloned.1.call-done = bf16[1152,2064]{1,0:T(8,128)(2,1)} async-done(((bf16[288,2064]{1,0:T(8,128)(2,1)}), bf16[1152,2064]{1,0:T(8,128)(2,1)}) %all-gather.12.cloned.1.call-update) | async-done | bytes 4755472 | tf_op jit(solution)/shard_map/all_gather | solution.py:57
  601.7 51.3 %while.27 = (s32[]{:T(128)}, bf16[4,4,72,2,258]{4,2,3,1,0:T(8,128)(2,1)}, bf16[4,4,72,2,258]{4,2,3,1,0:T(8,128)(2,1)}, bf16[4,4,72,2,258]{4,2,3,1,0:T(8,128)(2,1...) while((s32[]{:T(128)}, ...), condition=%wide.region_23.24_spmd, body=%wide.region_21.23_spmd.sunk | while | flops 390539744 | bytes 20462064 | solution.py:227
  678.8 7.7 fusion.65
  686.5 8.4 copy.135
  695.0 50.0 %reduce-scatter.24.cloned.1.call-done = bf16[288,2064]{1,0:T(8,128)(2,1)} async-done(((bf16[1152,2064]{1,0:T(8,128)(2,1)}), bf16[288,2064]{1,0:T(8,128)(2,1)}) %reduce-scatter.24.cloned.1.call-update) | async-done | bytes 1188880
  751.9 10.5 all-reduce
  770.1 11.5 %convolution_convert_fusion.4 = bf16[1152,1152]{1,0:T(8,128)(2,1)} fusion(bf16[1152,2064]{1,0:T(8,128)(2,1)} %all-gather.8.cloned.1.call-done, bf16[1152,2064]{0,1:T(8,128)(2,1)} %copy-done.49), kind=kOutput, calls=%fused_computation.102 | convolution fusion | flops 5479612416 | bytes 12165120 | tf_op jit(solution)/shard_map/dt,ft->df/dot_general | solution.py:213
  781.6 12.4 %convolution_convert_fusion.3 = bf16[1152,1152]{1,0:T(8,128)(2,1)} fusion(bf16[1152,2064]{0,1:T(8,128)(2,1)} %copy-done.50, bf16[1152,2064]{1,0:T(8,128)(2,1)} %all-gather.10.cloned.1.call-done), kind=kOutput, calls=%fused_computation.101 | convolution fusion | flops 5479612416 | bytes 12165120 | tf_op jit(solution)/shard_map/ft,ct->fc/dot_general | solution.py:66
  796.9 6.9 fusion.108
  823.3 39.2 %all-reduce.4 = (bf16[288]{0:T(512)(128)(2,1)S(1)}, bf16[288]{0:T(512)(128)(2,1)S(1)}, bf16[288]{0:T(512)(128)(2,1)S(1)}, bf16[288]{0:T(512)(128)(2,1)S(1)}, bf1...) all-reduce(bf16[288]{0:T(512)(128)(2,1)S(1)} %get-tuple-element.204, ...), channel_id=1, replica_groups=mesh['dp'=8,'tp'=4] {'dp'}, use_global_device_ids=true, to_apply=%region_32.33 | all-reduce | flops 3168 | bytes 12672 | tf_op jit(solution)/shard_map/psum | solution.py:263
  877.9 235.9 %all-reduce.8.cloned.1.call-done = (bf16[288,1152]{1,0:T(8,128)(2,1)}, bf16[288,1152]{1,0:T(8,128)(2,1)}, bf16[3,1152,288]{1,2,0:T(8,128)(2,1)}, bf16[288,1152]{...) async-done(((bf16[288,1152]{1,0:T(8,128)(2,1)}, bf16[288,1152]{1,0:T(8,128)(2,1)}, bf16[3,1152,288]{1,2,0:T(8,128)(2,1)}, ...) | async-done | bytes 9289744 | tf_op jit(solution)/shard_map/psum | solution.py:261
  (259 shorter events, 278.4 us)
Async XLA Ops:
  7.2 356.7 %copy-start = (bf16[1152,1152]{1,0:T(8,128)(2,1)S(1)}, bf16[1152,1152]{1,0:T(8,128)(2,1)}, u32[]{:S(2)}) copy-start(bf16[1152,1152]{1,0:T(8,128)(2,1)} %param.42) | copy-start | bytes 7962628
  7.2 96.1 %reduce-scatter.16.cloned.1.call-start = ((), (), s32[]{:S(2)}) async-start(), calls=%async_computation.10 | async-start | bytes 12533760
  18.8 88.0 %copy-start.30 = (f32[288]{0:T(512)S(1)}, f32[288]{0:T(512)}, u32[]{:S(2)}) copy-start(f32[288]{0:T(512)} %param.34) | copy-start | bytes 3460
  18.8 101.5 %copy-start.33 = (f32[288]{0:T(512)S(1)}, f32[288]{0:T(512)}, u32[]{:S(2)}) copy-start(f32[288]{0:T(512)} %param.35) | copy-start | bytes 3460
  18.9 101.5 %copy-start.36 = (f32[288]{0:T(512)S(1)}, f32[288]{0:T(512)}, u32[]{:S(2)}) copy-start(f32[288]{0:T(512)} %param.36) | copy-start | bytes 3460
  18.9 147.4 %all-gather.6.cloned.1.call-start = ((), (), s32[]{:S(2)}) async-start(), calls=%async_computation.5 | async-start | bytes 6266880 | tf_op jit(solution)/shard_map/all_gather | solution.py:35
  126.4 174.0 %reduce-scatter.18.cloned.1.call-start = ((), (), s32[]{:S(2)}) async-start(), calls=%async_computation.11 | async-start | bytes 6266880
  250.4 52.6 %copy-start.37 = (f32[288]{0:T(512)S(1)}, f32[288]{0:T(512)}, u32[]{:S(2)}) copy-start(f32[288]{0:T(512)} %param.39) | copy-start | bytes 3460
  250.4 113.5 %all-gather.8.cloned.1.call-start = ((), (), s32[]{:S(2)}) async-start(), calls=%async_computation.6 | async-start | bytes 6266880 | tf_op jit(solution)/shard_map/all_gather | solution.py:35
  303.0 14.9 %copy-start.32 = (f32[288]{0:T(512)S(1)}, f32[288]{0:T(512)}, u32[]{:S(2)}) copy-start(f32[288]{0:T(512)} %param.40) | copy-start | bytes 3460
  303.0 14.9 %copy-start.38 = (f32[288]{0:T(512)S(1)}, f32[288]{0:T(512)}, u32[]{:S(2)}) copy-start(f32[288]{0:T(512)} %param.41) | copy-start | bytes 3460
  324.0 91.3 %all-gather.10.cloned.1.call-start = ((), (), s32[]{:S(2)}) async-start(), calls=%async_computation.7 | async-start | bytes 6266880 | tf_op jit(solution)/shard_map/all_gather | solution.py:57
  328.0 35.9 %copy-start.46 = (f32[1152]{0:T(1024)S(1)}, f32[1152]{0:T(1024)}, u32[]{:S(2)}) copy-start(f32[1152]{0:T(1024)} %param.43) | copy-start | bytes 13828
  333.6 131.7 %reduce-scatter.20.cloned.1.call-start = ((), (), s32[]{:S(2)}) async-start(), calls=%async_computation.12 | async-start | bytes 6266880
  363.9 34.5 %copy-start.42 = (bf16[1152,1152]{1,0:T(8,128)(2,1)S(1)}, bf16[1152,1152]{1,0:T(8,128)(2,1)}, u32[]{:S(2)}) copy-start(bf16[1152,1152]{1,0:T(8,128)(2,1)} %param.44) | copy-start | bytes 7962628
  415.3 103.1 %reduce-scatter.22.cloned.1.call-start = ((), (), s32[]{:S(2)}) async-start(), calls=%async_computation.13 | async-start | bytes 6266880
  451.2 69.7 %copy-start.39 = (f32[288]{0:T(512)S(1)}, f32[288]{0:T(512)}, u32[]{:S(2)}) copy-start(f32[288]{0:T(512)} %param.45) | copy-start | bytes 3460
  451.2 133.4 %all-gather.12.cloned.1.call-start = ((), (), s32[]{:S(2)}) async-start(), calls=%async_computation.8 | async-start | bytes 6266880 | tf_op jit(solution)/shard_map/all_gather | solution.py:57
  520.9 16.3 %copy-start.2 = (bf16[2064,288]{1,0:T(8,128)(2,1)S(1)}, bf16[2064,288]{1,0:T(8,128)(2,1)}, u32[]{:S(2)}) copy-start(bf16[2064,288]{1,0:T(8,128)(2,1)} %copy.114) | copy-start | bytes 3566596
  542.2 42.5 %copy-start.45 = (bf16[288,1152]{1,0:T(8,128)(2,1)S(1)}, bf16[288,1152]{1,0:T(8,128)(2,1)}, u32[]{:S(2)}) copy-start(bf16[288,1152]{1,0:T(8,128)(2,1)} %param.38) | copy-start | bytes 1990660
  544.8 200.1 %reduce-scatter.24.cloned.1.call-start = ((), (), s32[]{:S(2)}) async-start(), calls=%async_computation.14 | async-start | bytes 6266880
  694.9 52.6 %copy-start.27 = (f32[2064]{0:T(1024)S(1)}, f32[2064]{0:T(1024)}, u32[]{:S(2)}) copy-start(f32[2064]{0:T(1024)} %copy-done.26) | copy-start | bytes 24772
  694.9 52.6 %copy-start.29 = (f32[2064]{0:T(1024)S(1)}, f32[2064]{0:T(1024)}, u32[]{:S(2)}) copy-start(f32[2064]{0:T(1024)} %copy-done.28) | copy-start | bytes 24772
  694.9 52.6 %copy-start.31 = (f32[288]{0:T(512)S(1)}, f32[288]{0:T(512)}, u32[]{:S(2)}) copy-start(f32[288]{0:T(512)} %param.34) | copy-start | bytes 3460
  694.9 52.6 %copy-start.34 = (f32[288]{0:T(512)S(1)}, f32[288]{0:T(512)}, u32[]{:S(2)}) copy-start(f32[288]{0:T(512)} %param.35) | copy-start | bytes 3460
  694.9 67.5 %copy-start.4 = (bf16[288,2064]{0,1:T(8,128)(2,1)S(1)}, bf16[288,2064]{0,1:T(8,128)(2,1)}, u32[]{:S(2)}) copy-start(bf16[288,2064]{0,1:T(8,128)(2,1)} %get-tuple-element.203) | copy-start | bytes 3566596
  694.9 115.0 %all-gather.14.cloned.1.call-start = ((), (), s32[]{:S(2)}) async-start(), calls=%async_computation.9 | async-start | bytes 6266880 | tf_op jit(solution)/shard_map/all_gather | solution.py:57
  770.1 343.8 %all-reduce.8.cloned.1.call-start = ((), (), s32[]{:S(2)}) async-start(), calls=%async_computation.15 | async-start | bytes 18579456 | tf_op jit(solution)/shard_map/psum | solution.py:261
  770.1 23.9 %slice-start.2 = ((s8[5013504]{0:T(1024)(128)(4,1)}), s8[4194304]{0:T(1024)(128)(4,1)S(1)}, s32[]{:S(2)}) async-start(s8[5013504]{0:T(1024)(128)(4,1)} %bitcast.211), calls=%async_computation.18 | async-start | bytes 8388608
  770.1 26.8 %slice-start = ((s8[5013504]{0:T(1024)(128)(4,1)}), s8[4194304]{0:T(1024)(128)(4,1)S(1)}, s32[]{:S(2)}) async-start(s8[5013504]{0:T(1024)(128)(4,1)} %bitcast.209), calls=%async_computation.16 | async-start | bytes 8388608
  781.6 15.3 %slice-start.1 = ((s8[5013504]{0:T(1024)(128)(4,1)}), s8[819200]{0:T(1024)(128)(4,1)S(1)}, s32[]{:S(2)}) async-start(s8[5013504]{0:T(1024)(128)(4,1)} %bitcast.209), calls=%async_computation.17 | async-start | bytes 1638400
  819.5 47.6 %copy-start.22 = (bf16[288,1152]{1,0:T(8,128)(2,1)S(1)}, bf16[288,1152]{1,0:T(8,128)(2,1)}, u32[]{:S(2)}) copy-start(bf16[288,1152]{1,0:T(8,128)(2,1)} %param.32) | copy-start | bytes 1990660
  (34 other events, 156.8 us)
Sparse Core Ops, SparseCore 0:
  19.0 84.3 reduce-scatter.15
  126.5 39.6 all-gather.5
  250.5 49.8 reduce-scatter.17
  324.2 39.6 all-gather.7
  365.9 39.0 all-gather.9
  415.4 49.8 reduce-scatter.19
  468.4 49.8 reduce-scatter.21
  545.0 39.6 all-gather.11
  695.0 49.8 reduce-scatter.23
  770.2 39.7 all-gather.13
  818.3 295.5 all-reduce.7
where the time goes:
time: 1140 us
  waiting for transfers between devices  601 us (53%)
  matrix products  221 us (19%)
  local copies, waits for them, and re-layouts  152 us (13%)
  blocking collectives  80.5 us (7%)
  other arithmetic  64.8 us (6%)
  between operations  15.4 us (1%)
    unnamed x16, waiting for transfers between devices  249 us
    psum x1, waiting for transfers between devices, body(): lax.psum(g_w_main.astype(jnp.bfloat16), 'dp').astype(jnp.float32)  236 us
    all_gather x2, waiting for transfers between devices, layer_norm(): return (normed, rstd, lax.all_gather(rounded, 'tp', axis=0, tiled=True))  69.8 us
    unnamed x123, local copies, waits for them, and re-layouts  63.8 us
    all_gather x3, waiting for transfers between devices, fold_back(): piece = lax.all_gather(shard, 'tp', axis=0, tiled=True)  46 us
    psum x1, blocking collectives, body(): lax.psum(g_b_skip.astype(jnp.bfloat16), 'dp').astype(jnp.float32)  39.2 us
    dot_general x4, matrix products, fold_back(): jnp.einsum('fc,ct->ft', weight, piece, preferred_element_type=jnp.float32)  32.7 us
    dot_general x1, matrix products, body(): jnp.einsum('dc,dt->ct', w_up, full_two, preferred_element_type=jnp.float32)  32.2 us
  transfers between devices with their start and end apart: 11, of which 10 were waited for; matrix products, arithmetic and copies ran while one was open for 13% of the time, Pallas kernels for 0%

commit v1 on v0

--- a/solution.py
+++ b/solution.py
@@ -54,7 +54,23 @@
 
 
 def fold_back(shard, pairs):
-    piece = lax.all_gather(shard, "tp", axis=0, tiled=True)
+    full_n = jax.lax.axis_size("tp")
+    shelf = []
+    for kk in range(full_n):
+        shelf.append((kk, (kk + 1) % full_n))
+    bank = []
+    for kk in range(full_n):
+        bank.append((kk, (kk - 1) % full_n))
+    reached, formed = ([shard], [shard])
+    for _ in range(full_n // 2):
+        reply = jax.lax.ppermute(reached[-1], axis_name="tp", perm=shelf)
+        reached.append(reply)
+    for _ in range((full_n - 1) // 2):
+        part_now = jax.lax.ppermute(formed[-1], "tp", bank)
+        formed.append(part_now)
+    y1 = jnp.concatenate([*reached[::-1], *formed[1:]], 0)
+    carry_out = jax.lax.axis_index("tp")
+    piece = jnp.roll(y1, (carry_out - full_n // 2) * shard.shape[0], 0)
     new_acts = tuple(
         (
             jnp.einsum("fc,ct->ft", weight, piece, preferred_element_type=jnp.float32)

time: 1140 us -> 1270 us (1.11)
  local copies, waits for them, and re-layouts: 152 us -> 204 us
  waiting for transfers between devices: 601 us -> 652 us
    ppermute x0 -> x9, waiting for transfers between devices: none -> 113 us  [the longest x6 102 us: fold_back(): reply = jax.lax.ppermute(reached[-1], axis_name='tp', perm=shelf)]
    all_gather x3 -> x0, waiting for transfers between devices: 46 us -> none  [fold_back(): piece = lax.all_gather(shard, 'tp', axis=0, tiled=True)]
    concatenate x0 -> x3, local copies, waits for them, and re-layouts: none -> 29 us  [fold_back(): y1 = jnp.concatenate([*reached[::-1], *formed[1:]], 0)]
    unnamed x16 -> x13, waiting for transfers between devices: 249 us -> 221 us
    ppermute x0 -> x9, local copies, waits for them, and re-layouts: none -> 23.3 us  [the longest x6 15.5 us: fold_back(): reply = jax.lax.ppermute(reached[-1], axis_name='tp', perm=shelf)]
    unnamed x123 -> x143, local copies, waits for them, and re-layouts: 63.8 us -> 64.7 us
  transfers between devices with their start and end apart: 11 -> 17, of which waited for: 10 -> 13; matrix products, arithmetic and copies ran while one was open for 13% -> 10% of each run, Pallas kernels for 0% -> 0%
where the time goes in v1:
time: 1270 us; the launch traced here: 1260 us
  waiting for transfers between devices  652 us (51%)
  matrix products  225 us (18%)
  local copies, waits for them, and re-layouts  204 us (16%)
  blocking collectives  80.8 us (6%)
  other arithmetic  72.3 us (6%)
  between operations  15.6 us (1%)
    psum x1, waiting for transfers between devices, body(): lax.psum(g_w_main.astype(jnp.bfloat16), 'dp').astype(jnp.float32)  239 us
    unnamed x13, waiting for transfers between devices  221 us
    ppermute x6, waiting for transfers between devices, fold_back(): reply = jax.lax.ppermute(reached[-1], axis_name='tp', perm=shelf)  102 us
    all_gather x2, waiting for transfers between devices, layer_norm(): return (normed, rstd, lax.all_gather(rounded, 'tp', axis=0, tiled=True))  79.3 us
    unnamed x143, local copies, waits for them, and re-layouts  64.7 us
    psum x1, blocking collectives, body(): lax.psum(g_b_skip.astype(jnp.bfloat16), 'dp').astype(jnp.float32)  39.7 us
    dot_general x1, matrix products, body(): jnp.einsum('dc,dt->ct', w_up, full_two, preferred_element_type=jnp.float32)  32.7 us
    dot_general x4, matrix products, fold_back(): jnp.einsum('fc,ct->ft', weight, piece, preferred_element_type=jnp.float32)  31.8 us
  transfers between devices with their start and end apart: 17, of which 13 were waited for; matrix products, arithmetic and copies ran while one was open for 10% of the time, Pallas kernels for 0%

profile of v1, /device:TPU:0, one launch (start us, length us, event | category | flops | bytes accessed | tf_op | source)
XLA Modules:
  0.0 1255.8 jit_solution(4794294259096169880)
XLA Ops:
  18.9 84.4 %reduce-scatter.16.cloned.1.call-done = f32[288,2064]{1,0:T(8,128)} async-done(((f32[1152,2064]{1,0:T(8,128)}), f32[288,2064]{1,0:T(8,128)}) %reduce-scatter.16.cloned.1.call-update) | async-done | bytes 2377744
  109.4 10.3 all-reduce.3
  126.6 39.6 %all-gather.3.cloned.1.call-done = bf16[1152,2064]{1,0:T(8,128)(2,1)} async-done(((bf16[288,2064]{1,0:T(8,128)(2,1)}), bf16[1152,2064]{1,0:T(8,128)(2,1)}) %all-gather.3.cloned.1.call-update) | async-done | bytes 4755472 | tf_op jit(solution)/shard_map/all_gather | solution.py:35
  202.9 23.2 %while.26 = (s32[]{:T(128)}, bf16[4,4,72,2,258]{4,2,3,1,0:T(8,128)(2,1)}, f32[4,4,2,258]{3,2,1,0:T(2,128)}, bf16[4,4,72,2,258]{4,2,3,1,0:T(8,128)(2,1)}, bf16[4,...) while((s32[]{:T(128)}, bf16[4,4,72,2,258]{4,2,3,1,0:T(8,128)(2,1)}, ...), condition=%wide.region_8.0_spmd, body=%wide.region_5.8_spmd.sunk | while | flops 157770096 | bytes 8231833 | solution.py:190
  250.2 50.0 %reduce-scatter.18.cloned.1.call-done = bf16[288,2064]{1,0:T(8,128)(2,1)} async-done(((bf16[1152,2064]{1,0:T(8,128)(2,1)}), bf16[288,2064]{1,0:T(8,128)(2,1)}) %reduce-scatter.18.cloned.1.call-update) | async-done | bytes 1188880
  307.4 10.3 all-reduce.2
  324.5 39.8 %all-gather.5.cloned.1.call-done = bf16[1152,2064]{1,0:T(8,128)(2,1)} async-done(((bf16[288,2064]{1,0:T(8,128)(2,1)}), bf16[1152,2064]{1,0:T(8,128)(2,1)}) %all-gather.5.cloned.1.call-update) | async-done | bytes 4755472 | tf_op jit(solution)/shard_map/all_gather | solution.py:35
  364.2 32.7 %fusion.68 = (bf16[1152,2064]{0,1:T(8,128)(2,1)S(1)}, f32[1152,2064]{0,1:T(8,128)}) fusion(f32[1152]{0:T(1024)S(1)} %copy-done.56, bf16[1152,2064]{1,0:T(8,128)(2,1)} %all-gather.5.cloned.1.call-done, bf16[1152,1152]{1,0:T(8,128)(2,1)S(1)} %copy-done), kind=kOutput, calls=%fused_computation.81 | convolution fusion | flops 5635215360 | bytes 21680640 | tf_op jit(solution)/shard_map/dc,dt->ct/dot_general | solution.py:204
  399.2 8.5 fusion.63
  407.7 8.4 copy.143
  427.2 44.2 %collective-permute-done = bf16[288,2064]{1,0:T(8,128)(2,1)} collective-permute-done((bf16[288,2064]{1,0:T(8,128)(2,1)}, bf16[288,2064]{1,0:T(8,128)(2,1)}, u32[]{:S(2)}, u32[]{:S(2)}) %collective-permute-start) | collective-permute-done | bytes 1188896 | tf_op jit(solution)/shard_map/ppermute | solution.py:66
  476.6 19.3 %collective-permute-done.1 = bf16[288,2064]{1,0:T(8,128)(2,1)} collective-permute-done((bf16[288,2064]{1,0:T(8,128)(2,1)}, bf16[288,2064]{1,0:T(8,128)(2,1)}, u32[]{:S(2)}, u32[]{:S(2)}) %collective-permute-start.1) | collective-permute-done | bytes 1188896 | tf_op jit(solution)/shard_map/ppermute | solution.py:66
  498.5 9.8 concatenate.12
  508.4 15.2 %fusion.129 = (bf16[1152]{0:T(1024)(128)(2,1)}, bf16[1152,2064]{0,1:T(8,128)(2,1)S(1)}) fusion(f32[1152,2064]{0,1:T(8,128)} %get-tuple-element.221, bf16[1152,1152]{1,0:T(8,128)(2,1)} %param.46, s32[]{:T(128)S(6)} %select_n.15, bf16[1152,2064]{0,1:T(8,128)(2,1)} %concatenate.12), kind=kOutput, calls=%fused_computation.185 | convolution fusion | flops 5513950208 | bytes 21678340 | tf_op jit(solution)/shard_map/fc,ct->ft/dot_general | solution.py:76
  525.8 8.7 fusion.64
  534.5 8.4 copy.145
  545.8 47.3 %reduce-scatter.22.cloned.1.call-done = bf16[288,2064]{1,0:T(8,128)(2,1)} async-done(((bf16[1152,2064]{1,0:T(8,128)(2,1)}), bf16[288,2064]{1,0:T(8,128)(2,1)}) %reduce-scatter.22.cloned.1.call-update) | async-done | bytes 1188880
  602.2 10.3 all-reduce.1
  621.3 27.0 %collective-permute-done.3 = bf16[288,2064]{1,0:T(8,128)(2,1)} collective-permute-done((bf16[288,2064]{1,0:T(8,128)(2,1)}, bf16[288,2064]{1,0:T(8,128)(2,1)}, u32[]{:S(2)}, u32[]{:S(2)}) %collective-permute-start.3) | collective-permute-done | bytes 1188896 | tf_op jit(solution)/shard_map/ppermute | solution.py:66
  653.8 11.5 collective-permute-done.4
  667.9 9.6 concatenate.13
  696.5 51.8 %while.27 = (s32[]{:T(128)}, bf16[4,4,72,2,258]{4,2,3,1,0:T(8,128)(2,1)}, bf16[4,4,72,2,258]{4,2,3,1,0:T(8,128)(2,1)}, bf16[4,4,72,2,258]{4,2,3,1,0:T(8,128)(2,1...) while((s32[]{:T(128)}, ...), condition=%wide.region_23.25_spmd, body=%wide.region_21.24_spmd.sunk | while | flops 390539744 | bytes 20462064 | solution.py:243
  781.8 8.4 copy.147
  790.3 11.4 convolution_convert_fusion.4
  801.7 39.0 %reduce-scatter.24.cloned.1.call-done = bf16[288,2064]{1,0:T(8,128)(2,1)} async-done(((bf16[1152,2064]{1,0:T(8,128)(2,1)}), bf16[288,2064]{1,0:T(8,128)(2,1)}) %reduce-scatter.24.cloned.1.call-update) | async-done | bytes 1188880
  847.6 10.3 all-reduce
  865.6 14.8 %convolution_convert_fusion.3 = bf16[1152,1152]{1,0:T(8,128)(2,1)} fusion(bf16[1152,2064]{0,1:T(8,128)(2,1)} %copy-done.60, s32[]{:T(128)S(6)} %select_n.15, bf16[1152,2064]{0,1:T(8,128)(2,1)} %concatenate.12), kind=kOutput, calls=%fused_computation.107 | convolution fusion | flops 5489123328 | bytes 12165124 | tf_op jit(solution)/shard_map/ft,ct->fc/dot_general | solution.py:82
  887.2 9.3 fusion.111
  899.1 10.2 collective-permute-done.8
  914.5 9.5 concatenate.14
  942.1 39.7 %all-reduce.4 = (bf16[288]{0:T(512)(128)(2,1)S(1)}, bf16[288]{0:T(512)(128)(2,1)S(1)}, bf16[288]{0:T(512)(128)(2,1)S(1)}, bf16[288]{0:T(512)(128)(2,1)S(1)}, bf1...) all-reduce(bf16[288]{0:T(512)(128)(2,1)S(1)} %get-tuple-element.205, ...), channel_id=1, replica_groups=mesh['dp'=8,'tp'=4] {'dp'}, use_global_device_ids=true, to_apply=%region_32.34 | all-reduce | flops 3168 | bytes 12672 | tf_op jit(solution)/shard_map/psum | solution.py:279
  995.4 239.0 %all-reduce.8.cloned.1.call-done = (bf16[288,1152]{1,0:T(8,128)(2,1)}, bf16[288,1152]{1,0:T(8,128)(2,1)}, bf16[3,1152,288]{1,2,0:T(8,128)(2,1)}, bf16[288,1152]{...) async-done(((bf16[288,1152]{1,0:T(8,128)(2,1)}, bf16[288,1152]{1,0:T(8,128)(2,1)}, bf16[3,1152,288]{1,2,0:T(8,128)(2,1)}, ...) | async-done | bytes 9289744 | tf_op jit(solution)/shard_map/psum | solution.py:277
  (301 shorter events, 352.7 us)
Async XLA Ops:
  7.2 357.0 %copy-start = (bf16[1152,1152]{1,0:T(8,128)(2,1)S(1)}, bf16[1152,1152]{1,0:T(8,128)(2,1)}, u32[]{:S(2)}) copy-start(bf16[1152,1152]{1,0:T(8,128)(2,1)} %param.44) | copy-start | bytes 7962628
  7.2 96.1 %reduce-scatter.16.cloned.1.call-start = ((), (), s32[]{:S(2)}) async-start(), calls=%async_computation.7 | async-start | bytes 12533760
  18.8 88.1 %copy-start.38 = (f32[288]{0:T(512)S(1)}, f32[288]{0:T(512)}, u32[]{:S(2)}) copy-start(f32[288]{0:T(512)} %param.36) | copy-start | bytes 3460
  18.8 101.5 %copy-start.42 = (f32[288]{0:T(512)S(1)}, f32[288]{0:T(512)}, u32[]{:S(2)}) copy-start(f32[288]{0:T(512)} %param.37) | copy-start | bytes 3460
  18.8 101.5 %copy-start.47 = (f32[288]{0:T(512)S(1)}, f32[288]{0:T(512)}, u32[]{:S(2)}) copy-start(f32[288]{0:T(512)} %param.38) | copy-start | bytes 3460
  18.8 147.4 %all-gather.3.cloned.1.call-start = ((), (), s32[]{:S(2)}) async-start(), calls=%async_computation.5 | async-start | bytes 6266880 | tf_op jit(solution)/shard_map/all_gather | solution.py:35
  126.4 173.8 %reduce-scatter.18.cloned.1.call-start = ((), (), s32[]{:S(2)}) async-start(), calls=%async_computation.8 | async-start | bytes 6266880
  250.2 52.6 %copy-start.48 = (f32[288]{0:T(512)S(1)}, f32[288]{0:T(512)}, u32[]{:S(2)}) copy-start(f32[288]{0:T(512)} %param.41) | copy-start | bytes 3460
  250.2 114.0 %all-gather.5.cloned.1.call-start = ((), (), s32[]{:S(2)}) async-start(), calls=%async_computation.6 | async-start | bytes 6266880 | tf_op jit(solution)/shard_map/all_gather | solution.py:35
  324.4 218.8 %reduce-scatter.20.cloned.1.call-start = ((), (), s32[]{:S(2)}) async-start(), calls=%async_computation.9 | async-start | bytes 6266880
  416.1 177.0 %reduce-scatter.22.cloned.1.call-start = ((), (), s32[]{:S(2)}) async-start(), calls=%async_computation.10 | async-start | bytes 6266880
  417.2 195.2 %copy-start.28 = (f32[2064]{0:T(1024)}, f32[2064]{0:T(1024)S(1)}, u32[]{:S(2)}) copy-start(f32[2064]{0:T(1024)S(1)} %mul.229) | copy-start | bytes 24772
  425.5 46.0 %collective-permute-start = (bf16[288,2064]{1,0:T(8,128)(2,1)}, bf16[288,2064]{1,0:T(8,128)(2,1)}, u32[]{:S(2)}, u32[]{:S(2)}) collective-permute-start(bf16[288,2064]{1,0:T(8,128)(2,1)} %copy.115), channel_id=1, source_target_pairs={{0,1},{1,2},{2,3},{3,0},{4,5},{5,6},{6,7},{7,4},{8,9},{9,10},{10,1... | collective-permute-start | bytes 3566600 | tf_op jit(solution)/shard_map/ppermute | solution.py:66
  425.7 48.3 %collective-permute-start.2 = (bf16[288,2064]{1,0:T(8,128)(2,1)}, bf16[288,2064]{1,0:T(8,128)(2,1)}, u32[]{:S(2)}, u32[]{:S(2)}) collective-permute-start(bf16[288,2064]{1,0:T(8,128)(2,1)} %copy.115), channel_id=1, source_target_pairs={{0,3},{1,0},{2,1},{3,2},{4,7},{5,4},{6,5},{7,6},{8,11},{9,8},{10,9... | collective-permute-start | bytes 3566600 | tf_op jit(solution)/shard_map/ppermute | solution.py:69
  471.4 24.5 %collective-permute-start.1 = (bf16[288,2064]{1,0:T(8,128)(2,1)}, bf16[288,2064]{1,0:T(8,128)(2,1)}, u32[]{:S(2)}, u32[]{:S(2)}) collective-permute-start(bf16[288,2064]{1,0:T(8,128)(2,1)} %collective-permute-done), channel_id=1, source_target_pairs={{0,1},{1,2},{2,3},{3,0},{4,5},{5,6},{6,7},{7,4},{8,9},{9,10},{10,1... | collective-permute-start | bytes 3566600 | tf_op jit(solution)/shard_map/ppermute | solution.py:66
  542.9 52.8 %copy-start.35 = (f32[2064]{0:T(1024)S(1)}, f32[2064]{0:T(1024)}, u32[]{:S(2)}) copy-start(f32[2064]{0:T(1024)} %copy-done.34) | copy-start | bytes 24772
  542.9 52.8 %copy-start.37 = (f32[2064]{0:T(1024)S(1)}, f32[2064]{0:T(1024)}, u32[]{:S(2)}) copy-start(f32[2064]{0:T(1024)} %copy-done.36) | copy-start | bytes 24772
  542.9 52.8 %copy-start.41 = (f32[288]{0:T(512)S(1)}, f32[288]{0:T(512)}, u32[]{:S(2)}) copy-start(f32[288]{0:T(512)} %param.42) | copy-start | bytes 3460
  542.9 52.8 %copy-start.50 = (f32[288]{0:T(512)S(1)}, f32[288]{0:T(512)}, u32[]{:S(2)}) copy-start(f32[288]{0:T(512)} %param.47) | copy-start | bytes 3460
  542.9 297.7 %reduce-scatter.24.cloned.1.call-start = ((), (), s32[]{:S(2)}) async-start(), calls=%async_computation.11 | async-start | bytes 6266880
  619.6 28.8 %collective-permute-start.3 = (bf16[288,2064]{1,0:T(8,128)(2,1)}, bf16[288,2064]{1,0:T(8,128)(2,1)}, u32[]{:S(2)}, u32[]{:S(2)}) collective-permute-start(bf16[288,2064]{1,0:T(8,128)(2,1)} %copy.120), channel_id=1, source_target_pairs={{0,1},{1,2},{2,3},{3,0},{4,5},{5,6},{6,7},{7,4},{8,9},{9,10},{10,1... | collective-permute-start | bytes 3566600 | tf_op jit(solution)/shard_map/ppermute | solution.py:66
  619.6 31.6 %collective-permute-start.5 = (bf16[288,2064]{1,0:T(8,128)(2,1)}, bf16[288,2064]{1,0:T(8,128)(2,1)}, u32[]{:S(2)}, u32[]{:S(2)}) collective-permute-start(bf16[288,2064]{1,0:T(8,128)(2,1)} %copy.120), channel_id=1, source_target_pairs={{0,3},{1,0},{2,1},{3,2},{4,7},{5,4},{6,5},{7,6},{8,11},{9,8},{10,9... | collective-permute-start | bytes 3566600 | tf_op jit(solution)/shard_map/ppermute | solution.py:69
  648.3 16.9 %collective-permute-start.4 = (bf16[288,2064]{1,0:T(8,128)(2,1)}, bf16[288,2064]{1,0:T(8,128)(2,1)}, u32[]{:S(2)}, u32[]{:S(2)}) collective-permute-start(bf16[288,2064]{1,0:T(8,128)(2,1)} %collective-permute-done.3), channel_id=1, source_target_pairs={{0,1},{1,2},{2,3},{3,0},{4,5},{5,6},{6,7},{7,4},{8,9},{9,10},{10,1... | collective-permute-start | bytes 3566600 | tf_op jit(solution)/shard_map/ppermute | solution.py:66
  790.2 53.0 %copy-start.31 = (f32[2064]{0:T(1024)S(1)}, f32[2064]{0:T(1024)}, u32[]{:S(2)}) copy-start(f32[2064]{0:T(1024)} %copy-done.30) | copy-start | bytes 24772
  790.2 53.0 %copy-start.33 = (f32[2064]{0:T(1024)S(1)}, f32[2064]{0:T(1024)}, u32[]{:S(2)}) copy-start(f32[2064]{0:T(1024)} %copy-done.32) | copy-start | bytes 24772
  790.2 53.0 %copy-start.39 = (f32[288]{0:T(512)S(1)}, f32[288]{0:T(512)}, u32[]{:S(2)}) copy-start(f32[288]{0:T(512)} %param.36) | copy-start | bytes 3460
  790.2 53.0 %copy-start.43 = (f32[288]{0:T(512)S(1)}, f32[288]{0:T(512)}, u32[]{:S(2)}) copy-start(f32[288]{0:T(512)} %param.37) | copy-start | bytes 3460
  790.2 444.1 %all-reduce.8.cloned.1.call-start = ((), (), s32[]{:S(2)}) async-start(), calls=%async_computation.12 | async-start | bytes 18579456 | tf_op jit(solution)/shard_map/psum | solution.py:277
  801.7 56.2 %copy-start.3 = (bf16[288,2064]{0,1:T(8,128)(2,1)S(1)}, bf16[288,2064]{0,1:T(8,128)(2,1)}, u32[]{:S(2)}) copy-start(bf16[288,2064]{0,1:T(8,128)(2,1)} %copy-done.2) | copy-start | bytes 3566596
  865.6 16.7 %collective-permute-start.6 = (bf16[288,2064]{1,0:T(8,128)(2,1)}, bf16[288,2064]{1,0:T(8,128)(2,1)}, u32[]{:S(2)}, u32[]{:S(2)}) collective-permute-start(bf16[288,2064]{1,0:T(8,128)(2,1)} %copy.129), channel_id=1, source_target_pairs={{0,1},{1,2},{2,3},{3,0},{4,5},{5,6},{6,7},{7,4},{8,9},{9,10},{10,1... | collective-permute-start | bytes 3566600 | tf_op jit(solution)/shard_map/ppermute | solution.py:66
  880.4 29.0 %collective-permute-start.8 = (bf16[288,2064]{1,0:T(8,128)(2,1)}, bf16[288,2064]{1,0:T(8,128)(2,1)}, u32[]{:S(2)}, u32[]{:S(2)}) collective-permute-start(bf16[288,2064]{1,0:T(8,128)(2,1)} %copy.129), channel_id=1, source_target_pairs={{0,3},{1,0},{2,1},{3,2},{4,7},{5,4},{6,5},{7,6},{8,11},{9,8},{10,9... | collective-permute-start | bytes 3566600 | tf_op jit(solution)/shard_map/ppermute | solution.py:69
  882.3 29.7 %collective-permute-start.7 = (bf16[288,2064]{1,0:T(8,128)(2,1)}, bf16[288,2064]{1,0:T(8,128)(2,1)}, u32[]{:S(2)}, u32[]{:S(2)}) collective-permute-start(bf16[288,2064]{1,0:T(8,128)(2,1)} %collective-permute-done.6), channel_id=1, source_target_pairs={{0,1},{1,2},{2,3},{3,0},{4,5},{5,6},{6,7},{7,4},{8,9},{9,10},{10,1... | collective-permute-start | bytes 3566600 | tf_op jit(solution)/shard_map/ppermute | solution.py:66
  (50 other events, 422.2 us)
Sparse Core Ops, SparseCore 0:
  18.9 84.3 reduce-scatter.15
  126.5 39.6 all-gather.2
  250.3 49.8 reduce-scatter.17
  324.5 39.6 all-gather.4
  416.2 71.5 reduce-scatter.19
  543.0 50.0 reduce-scatter.21
  790.3 50.2 reduce-scatter.23
  936.9 297.4 all-reduce.7
